TPU v7x, 32 devices: a whole 2x2x4 slice. The times are simulated.
32 devices in a mesh: rows: 8 (over z, x), cols: 4 (over y, core).
Axes of the slice: x: 2, y: 2, z: 4, core: 2. Of those that a mesh axis runs over, the one named last changes fastest.
Arguments:
- basis: float32 [8192, 4096], P('rows', 'cols'), may hold values from -119.66257 to 119.66257, as said below
- block: float32 [8192, 512], P('rows', 'cols'), may hold values from -1800 to 1800
Outputs:
- ortho: float32 [8192, 512], P('rows', 'cols')
- factors: float32 [4, 128, 128], P('cols')
Inputs may be any that keep to these rules, and one draw needn't show every extreme that they name: Under the inner product (sum over rows divided by 8192) the basis columns have squared norms between 0.6 and 1.9, and inner products of distinct basis columns are at most 0.05 in magnitude.
All inputs are finite; a program needn't handle non-finite values.
Results may differ from a plain program's by a relative error of at most 0.000076.
Values sent between devices are 32-bit elements; how exact they have to be, the bound alone decides.
No kernel may reach another device: no remote copies, remote signals or barrier semaphores. Data moves between devices by JAX's collectives and lax.ppermute only.
A program may use at most 64 MiB of HBM per device.

v0:
```python
import jax
import jax.numpy as jnp
from jax import lax
from jax.sharding import PartitionSpec as P

BLK = 128


def solve_block(lower_factor, vectors):
    return jax.scipy.linalg.solve_triangular(lower_factor, vectors, lower=True)


def body(basis, block):
    highest = lax.Precision.HIGHEST
    local_rows = basis.shape[0]
    inverse = 1.0 / (local_rows * lax.axis_size("rows"))
    width = block.shape[1]
    column_index = lax.axis_index("cols")

    def project(piece):
        return (
            lax.dot_general(
                basis,
                piece,
                (((0,), (0,)), ((), ())),
                precision=highest,
                preferred_element_type=jnp.float32,
            )
            * inverse
        )

    def expand(coef):
        return jnp.dot(basis, coef, precision=highest, preferred_element_type=jnp.float32)

    terms_one = project(lax.all_gather(block, "cols", axis=1, tiled=True))
    coef_one = lax.psum(terms_one, "rows")
    placed = lax.dynamic_update_slice_in_dim(
        jnp.zeros((local_rows, coef_one.shape[1]), jnp.float32), block, column_index * width, 1
    )
    first_whole = lax.psum(placed - expand(coef_one), "cols")
    terms_two = project(first_whole)
    first = lax.dynamic_slice_in_dim(first_whole, column_index * width, width, 1)
    coef_two = lax.psum(terms_two, "rows")
    second = first - lax.psum_scatter(expand(coef_two), "cols", scatter_dimension=1, tiled=True)
    blocks = width // BLK
    pieces = second.reshape(local_rows, blocks, BLK)
    gram = jnp.einsum("mbi,mbj->bij", pieces, pieces, precision=highest) * inverse
    gram = lax.psum(gram, "rows")
    lower_factor = jnp.linalg.cholesky(gram)
    solved = jax.vmap(solve_block)(lower_factor, jnp.transpose(pieces, (1, 2, 0)))
    ortho = jnp.transpose(solved, (2, 0, 1)).reshape(local_rows, width)
    return (ortho, jnp.transpose(lower_factor, (0, 2, 1)))


def solution(mesh):
    placed = (P("rows", "cols"), P("rows", "cols"))
    return jax.shard_map(
        body,
        mesh=mesh,
        in_specs=placed,
        out_specs=(P("rows", "cols"), P("cols", None, None)),
        check_vma=False,
    )
```

profile of v0, /device:TPU:0, one launch (start us, length us, event | category | flops | bytes accessed | tf_op | source)
XLA Modules:
  0.0 476.0 jit_solution(7517272405939530119)
XLA Ops:
  7.2 0.0 all-gather.2.cloned.1.call-start
  7.2 0.7 all-gather.2.cloned.1.call-update
  7.9 0.0 all-reduce.5.cloned.1.call-start
  7.9 27.2 %all-gather.2.cloned.1.call-done = f32[1024,512]{1,0:T(8,128)} async-done(((f32[1024,128]{1,0:T(8,128)}), f32[1024,512]{1,0:T(8,128)}) %all-gather.2.cloned.1.call-update) | async-done | bytes 2097168 | tf_op jit(solution)/shard_map/all_gather | solution.py:35
  35.1 10.2 %convolution_multiply_fusion = f32[1024,512]{1,0:T(8,128)} fusion(f32[1024,1024]{1,0:T(8,128)} %param.2, f32[1024,512]{1,0:T(8,128)} %all-gather.2.cloned.1.call-done), kind=kOutput, calls=%fused_computation.3 | convolution fusion | flops 6442975232 | bytes 8388608 | tf_op jit(solution)/shard_map/dot_general | solution.py:22
  45.3 0.0 all-reduce.5.cloned.1.call-update
  45.3 0.0 all-reduce.7.cloned.1.call-start
  45.4 1.0 copy-done.1
  46.3 0.2 copy.4
  46.5 0.2 broadcast_in_dim.7
  46.8 0.1 constant_dynamic-update-slice_fusion
  46.8 100.9 %all-reduce.5.cloned.1.call-done = f32[1024,512]{1,0:T(8,128)} async-done(((f32[1024,512]{1,0:T(8,128)}), f32[1024,512]{1,0:T(8,128)}) %all-reduce.5.cloned.1.call-update) | async-done | bytes 2097168 | tf_op jit(solution)/shard_map/psum | solution.py:36
  147.8 16.7 %bitcast_subtract_fusion = f32[1024,512]{0,1:T(8,128)} fusion(f32[1024,512]{0,1:T(8,128)S(1)} %constant_dynamic-update-slice_fusion, f32[1024,512]{1,0:T(8,128)} %all-reduce.5.cloned.1.call-done, f32[1024,1024]{1,0:T(8,128)} %param.2), kind=kOutput, calls=%fused_computation | convolution fusion | flops 6442975232 | bytes 10485760 | tf_op jit(solution)/shard_map/dot_general | solution.py:33
  164.5 0.2 all-reduce.9.cloned.1.call-start
  164.7 50.6 %all-reduce.7.cloned.1.call-done = f32[1024,512]{0,1:T(8,128)} async-done(((f32[1024,512]{0,1:T(8,128)}), f32[1024,512]{0,1:T(8,128)}) %all-reduce.7.cloned.1.call-update) | async-done | bytes 2097168 | tf_op jit(solution)/shard_map/psum | solution.py:40
  215.3 10.2 %multiply_bitcast_fusion = f32[1024,512]{0,1:T(8,128)} fusion(f32[1024,512]{0,1:T(8,128)} %all-reduce.7.cloned.1.call-done, f32[1024,1024]{1,0:T(8,128)} %param.2), kind=kOutput, calls=%fused_computation.1 | convolution fusion | flops 6442975232 | bytes 8388608 | tf_op jit(solution)/shard_map/dot_general | solution.py:22
  225.6 0.0 reduce-scatter.2.cloned.1.call-start
  225.6 102.5 %all-reduce.9.cloned.1.call-done = f32[1024,512]{0,1:T(8,128)} async-done(((f32[1024,512]{0,1:T(8,128)}), f32[1024,512]{0,1:T(8,128)}) %all-reduce.9.cloned.1.call-update) | async-done | bytes 2097168 | tf_op jit(solution)/shard_map/psum | solution.py:43
  328.1 10.3 %convolution_bitcast_fusion = f32[1024,512]{0,1:T(8,128)} fusion(f32[1024,512]{0,1:T(8,128)} %all-reduce.9.cloned.1.call-done, f32[1024,1024]{1,0:T(8,128)} %param.2), kind=kOutput, calls=%fused_computation.2 | convolution fusion | flops 6442450944 | bytes 8388608 | tf_op jit(solution)/shard_map/dot_general | solution.py:33
  338.4 0.3 all-reduce.11.cloned.1.call-start
  338.7 30.3 %reduce-scatter.2.cloned.1.call-done = f32[1024,128]{0,1:T(8,128)} async-done(((f32[1024,512]{0,1:T(8,128)}), f32[1024,128]{0,1:T(8,128)}) %reduce-scatter.2.cloned.1.call-update) | async-done | bytes 524304 | tf_op jit(solution)/shard_map/reduce_scatter | solution.py:44
  369.0 2.5 fusion
  371.5 70.6 %all-reduce.11.cloned.1.call-done = f32[1,128,128]{1,2,0:T(8,128)} async-done(((f32[1,128,128]{1,2,0:T(8,128)}), f32[1,128,128]{1,2,0:T(8,128)}) %all-reduce.11.cloned.1.call-update) | async-done | bytes 65552 | tf_op jit(solution)/shard_map/psum | solution.py:48
  442.2 0.9 copy.6
  443.1 0.9 fusion.3
  444.0 11.7 %custom-call.8 = f32[1,128,128]{2,1,0:T(8,128)S(1)} custom-call(f32[1,128,128]{2,1,0:T(8,128)S(1)} %fusion.3), custom_call_target="Cholesky" | custom-call | tf_op jit(solution)/shard_map/jit(cholesky)/cholesky | solution.py:49
  455.7 0.6 compare_reduce_fusion
  456.4 0.7 fusion.4
  457.0 9.8 %custom-call.9 = f32[1,1,128,128]{2,3,1,0:T(8,128)S(1)} custom-call(f32[1,1,128,128]{3,2,1,0:T(8,128)S(1)} %get-tuple-element.5), custom_call_target="InvertDiagBlocksLowerTriangular" | custom-call | tf_op jit(solution)/shard_map/vmap(jit(_solve_triangular))/triangular_solve | solution.py:10
  466.8 0.6 convolution_bitcast_fusion.1
  467.5 1.0 copy.7
  468.5 0.7 copy.8
  (10 shorter events, 0.1 us)
Async XLA Ops:
  7.2 27.9 %all-gather.2.cloned.1.call-start = ((), (), s32[]{:S(2)}) async-start(), calls=%async_computation.1 | async-start | bytes 2621440 | tf_op jit(solution)/shard_map/all_gather | solution.py:35
  7.9 139.9 %all-reduce.5.cloned.1.call-start = ((), (), s32[]{:S(2)}) async-start(), calls=%async_computation.2 | async-start | bytes 4194304 | tf_op jit(solution)/shard_map/psum | solution.py:36
  45.3 1.0 copy-start.1
  45.3 170.0 %all-reduce.7.cloned.1.call-start = ((), (), s32[]{:S(2)}) async-start(), calls=%async_computation.3 | async-start | bytes 4194304 | tf_op jit(solution)/shard_map/psum | solution.py:40
  164.5 163.6 %all-reduce.9.cloned.1.call-start = ((), (), s32[]{:S(2)}) async-start(), calls=%async_computation.4 | async-start | bytes 4194304 | tf_op jit(solution)/shard_map/psum | solution.py:43
  225.6 143.4 %reduce-scatter.2.cloned.1.call-start = ((), (), s32[]{:S(2)}) async-start(), calls=%async_computation.5 | async-start | bytes 2621440 | tf_op jit(solution)/shard_map/reduce_scatter | solution.py:44
  338.4 30.6 %copy-start = (f32[1024,512]{0,1:T(8,128)S(1)}, f32[1024,512]{0,1:T(8,128)}, u32[]{:S(2)}) copy-start(f32[1024,512]{0,1:T(8,128)} %all-reduce.7.cloned.1.call-done) | copy-start | bytes 6291460
  338.4 103.8 %all-reduce.11.cloned.1.call-start = ((), (), s32[]{:S(2)}) async-start(), calls=%async_computation.6 | async-start | bytes 131072 | tf_op jit(solution)/shard_map/psum | solution.py:48
  369.0 97.8 %copy-start.2 = (f32[1024,128]{0,1:T(8,128)S(1)}, f32[1024,128]{0,1:T(8,128)}, u32[]{:S(2)}) copy-start(f32[1024,128]{0,1:T(8,128)} %reduce-scatter.2.cloned.1.call-done) | copy-start | bytes 1572868
Sparse Core Ops, SparseCore 0:
  9.5 25.5 all-gather.1
  45.4 102.3 all-reduce.4
  164.6 50.6 all-reduce.6
  225.7 102.3 all-reduce.8
  338.5 30.4 reduce-scatter.1
  372.9 69.2 all-reduce.10
where the time goes:
time: 476 us
  waiting for transfers between devices  383 us (80%)
  matrix products  50.5 us (11%)
  other arithmetic  23.7 us (5%)
  between operations  14.2 us (3%)
    psum x1, waiting for transfers between devices, body(): coef_two = lax.psum(terms_two, 'rows')  102 us
    psum x1, waiting for transfers between devices, body(): coef_one = lax.psum(terms_one, 'rows')  101 us
    psum x1, waiting for transfers between devices, body(): gram = lax.psum(gram, 'rows')  70.6 us
    psum x1, waiting for transfers between devices, body(): first_whole = lax.psum(placed - expand(coef_one), 'cols')  50.6 us
    reduce_scatter x1, waiting for transfers between devices, body(): lax.psum_scatter(expand(coef_two), 'cols', scatter_dimension=1, tiled=True)  30.3 us
    all_gather x1, waiting for transfers between devices, body(): terms_one = project(lax.all_gather(block, 'cols', axis=1, tiled=True))  27.2 us
    dot_general x2, matrix products, expand(): jnp.dot(basis, coef, precision=highest, preferred_element_type=jnp.float32)  27 us
    dot_general x2, matrix products, project(): lax.dot_general(basis, piece, (((0,), (0,)), ((), ())), precision=highest...  20.4 us
  transfers between devices with their start and end apart: 6, of which 6 were waited for; matrix products, arithmetic and copies ran while one was open for 0% of the time, Pallas kernels for 0%

commit v1 on v0

--- a/solution.py
+++ b/solution.py
@@ -4,6 +4,14 @@
 from jax.sharding import PartitionSpec as P
 
 BLK = 128
+
+
+def add_in_pairs(block, axis):
+    size, total = (lax.axis_size(axis), block)
+    for reach in [1 << k for k in range(size.bit_length() - 1)]:
+        swap = [(i, i ^ reach) for i in range(size)]
+        total = total + lax.ppermute(total, axis, swap)
+    return total
 
 
 def solve_block(lower_factor, vectors):
@@ -40,7 +48,7 @@
     first_whole = lax.psum(placed - expand(coef_one), "cols")
     terms_two = project(first_whole)
     first = lax.dynamic_slice_in_dim(first_whole, column_index * width, width, 1)
-    coef_two = lax.psum(terms_two, "rows")
+    coef_two = add_in_pairs(terms_two, "rows")
     second = first - lax.psum_scatter(expand(coef_two), "cols", scatter_dimension=1, tiled=True)
     blocks = width // BLK
     pieces = second.reshape(local_rows, blocks, BLK)

time: 476 us -> 558 us (1.17)
  waiting for transfers between devices: 383 us -> 461 us
    ppermute x0 -> x3, waiting for transfers between devices: none -> 179 us  [add_in_pairs(): total = total + lax.ppermute(total, axis, swap)]
    psum x1 -> x0, waiting for transfers between devices: 102 us -> none  [body(): coef_two = lax.psum(terms_two, 'rows')]
  transfers between devices with their start and end apart: 6 -> 8, of which waited for: 6 -> 8; matrix products, arithmetic and copies ran while one was open for 0% -> 0% of each run, Pallas kernels for 0% -> 0%
where the time goes in v1:
time: 558 us
  waiting for transfers between devices  461 us (83%)
  matrix products  47.9 us (9%)
  other arithmetic  24.7 us (4%)
  between operations  13.9 us (2%)
  starting transfers between devices  6.16 us (1%)
    ppermute x3, waiting for transfers between devices, add_in_pairs(): total = total + lax.ppermute(total, axis, swap)  179 us
    psum x1, waiting for transfers between devices, body(): coef_one = lax.psum(terms_one, 'rows')  101 us
    psum x1, waiting for transfers between devices, body(): gram = lax.psum(gram, 'rows')  70.6 us
    psum x1, waiting for transfers between devices, body(): first_whole = lax.psum(placed - expand(coef_one), 'cols')  50.6 us
    reduce_scatter x1, waiting for transfers between devices, body(): lax.psum_scatter(expand(coef_two), 'cols', scatter_dimension=1, tiled=True)  31.5 us
    all_gather x1, waiting for transfers between devices, body(): terms_one = project(lax.all_gather(block, 'cols', axis=1, tiled=True))  27.2 us
    dot_general x2, matrix products, expand(): jnp.dot(basis, coef, precision=highest, preferred_element_type=jnp.float32)  24.9 us
    dot_general x2, matrix products, project(): lax.dot_general(basis, piece, (((0,), (0,)), ((), ())), precision=highest...  19.8 us
  transfers between devices with their start and end apart: 8, of which 8 were waited for; matrix products, arithmetic and copies ran while one was open for 0% of the time, Pallas kernels for 0%

profile of v1, /device:TPU:0, one launch (start us, length us, event | category | flops | bytes accessed | tf_op | source)
XLA Modules:
  0.0 557.5 jit_solution(7867512145712575013)
XLA Ops:
  7.2 0.7 all-gather.2.cloned.1.call-update
  7.9 27.2 %all-gather.2.cloned.1.call-done = f32[1024,512]{1,0:T(8,128)} async-done(((f32[1024,128]{1,0:T(8,128)}), f32[1024,512]{1,0:T(8,128)}) %all-gather.2.cloned.1.call-update) | async-done | bytes 2097168 | tf_op jit(solution)/shard_map/all_gather | solution.py:43
  35.1 10.2 %convolution_multiply_fusion = f32[1024,512]{1,0:T(8,128)} fusion(f32[1024,1024]{1,0:T(8,128)} %param.2, f32[1024,512]{1,0:T(8,128)} %all-gather.2.cloned.1.call-done), kind=kOutput, calls=%fused_computation.5 | convolution fusion | flops 6442975232 | bytes 8388608 | tf_op jit(solution)/shard_map/dot_general | solution.py:30
  45.4 1.0 copy-done.2
  46.5 0.2 broadcast_in_dim.7
  46.8 100.9 %all-reduce.4.cloned.1.call-done = f32[1024,512]{1,0:T(8,128)} async-done(((f32[1024,512]{1,0:T(8,128)}), f32[1024,512]{1,0:T(8,128)}) %all-reduce.4.cloned.1.call-update) | async-done | bytes 2097168 | tf_op jit(solution)/shard_map/psum | solution.py:44
  147.8 16.7 %bitcast_subtract_fusion = f32[1024,512]{0,1:T(8,128)} fusion(f32[1024,512]{0,1:T(8,128)S(1)} %constant_dynamic-update-slice_fusion, f32[1024,512]{1,0:T(8,128)} %all-reduce.4.cloned.1.call-done, f32[1024,1024]{1,0:T(8,128)} %param.2), kind=kOutput, calls=%fused_computation | convolution fusion | flops 6442975232 | bytes 10485760 | tf_op jit(solution)/shard_map/dot_general | solution.py:41
  164.5 0.2 reduce-scatter.2.cloned.1.call-start
  164.7 50.6 %all-reduce.6.cloned.1.call-done = f32[1024,512]{0,1:T(8,128)} async-done(((f32[1024,512]{0,1:T(8,128)}), f32[1024,512]{0,1:T(8,128)}) %all-reduce.6.cloned.1.call-update) | async-done | bytes 2097168 | tf_op jit(solution)/shard_map/psum | solution.py:48
  215.3 9.7 %multiply_bitcast_fusion = f32[1024,512]{0,1:T(8,128)S(1)} fusion(f32[1024,512]{0,1:T(8,128)} %all-reduce.6.cloned.1.call-done, f32[1024,1024]{1,0:T(8,128)} %param.2), kind=kOutput, calls=%fused_computation.3 | convolution fusion | flops 6442975232 | bytes 8388608 | tf_op jit(solution)/shard_map/dot_general | solution.py:30
  225.0 1.5 collective-permute-start
  226.5 45.7 %collective-permute-done = f32[1024,512]{0,1:T(8,128)S(1)} collective-permute-done((f32[1024,512]{0,1:T(8,128)S(1)}, f32[1024,512]{0,1:T(8,128)S(1)}, u32[]{:S(2)}, u32[]{:S(2)}) %collective-permute-start) | collective-permute-done | bytes 2097184 | tf_op jit(solution)/shard_map/ppermute | solution.py:13
  272.2 0.6 add.34
  272.7 1.5 collective-permute-start.1
  274.3 44.8 %collective-permute-done.1 = f32[1024,512]{0,1:T(8,128)S(1)} collective-permute-done((f32[1024,512]{0,1:T(8,128)S(1)}, f32[1024,512]{0,1:T(8,128)S(1)}, u32[]{:S(2)}, u32[]{:S(2)}) %collective-permute-start.1) | collective-permute-done | bytes 2097184 | tf_op jit(solution)/shard_map/ppermute | solution.py:13
  319.1 0.4 add.35
  319.5 2.5 collective-permute-start.2
  322.0 88.9 %collective-permute-done.2 = f32[1024,512]{0,1:T(8,128)S(1)} collective-permute-done((f32[1024,512]{0,1:T(8,128)S(1)}, f32[1024,512]{0,1:T(8,128)S(1)}, u32[]{:S(2)}, u32[]{:S(2)}) %collective-permute-start.2) | collective-permute-done | bytes 2097184 | tf_op jit(solution)/shard_map/ppermute | solution.py:13
  410.9 8.2 %fusion.2 = f32[1024,512]{0,1:T(8,128)} fusion(f32[1024,1024]{1,0:T(8,128)S(1)} %copy-done, f32[1024,512]{0,1:T(8,128)S(1)} %add.35, f32[1024,512]{0,1:T(8,128)S(1)} %collective-permute-done.2), kind=kOutput, calls=%fused_computation.4 | convolution fusion | flops 6442975232 | bytes 10485760 | tf_op jit(solution)/shard_map/dot_general | solution.py:41
  419.1 0.3 all-reduce.8.cloned.1.call-start
  419.4 31.5 %reduce-scatter.2.cloned.1.call-done = f32[1024,128]{0,1:T(8,128)} async-done(((f32[1024,512]{0,1:T(8,128)}), f32[1024,128]{0,1:T(8,128)}) %reduce-scatter.2.cloned.1.call-update) | async-done | bytes 524304 | tf_op jit(solution)/shard_map/reduce_scatter | solution.py:52
  450.9 2.5 fusion.5
  453.4 70.6 %all-reduce.8.cloned.1.call-done = f32[1,128,128]{1,2,0:T(8,128)} async-done(((f32[1,128,128]{1,2,0:T(8,128)}), f32[1,128,128]{1,2,0:T(8,128)}) %all-reduce.8.cloned.1.call-update) | async-done | bytes 65552 | tf_op jit(solution)/shard_map/psum | solution.py:56
  524.0 0.9 copy.6
  524.9 0.9 fusion.8
  525.8 11.7 %custom-call.8 = f32[1,128,128]{2,1,0:T(8,128)S(1)} custom-call(f32[1,128,128]{2,1,0:T(8,128)S(1)} %fusion.8), custom_call_target="Cholesky" | custom-call | tf_op jit(solution)/shard_map/jit(cholesky)/cholesky | solution.py:57
  537.5 0.6 compare_reduce_fusion
  538.2 0.7 fusion.9
  538.8 0.7 copy.8
  539.6 9.8 %custom-call.9 = f32[1,1,128,128]{2,3,1,0:T(8,128)S(1)} custom-call(f32[1,1,128,128]{3,2,1,0:T(8,128)S(1)} %get-tuple-element.5), custom_call_target="InvertDiagBlocksLowerTriangular" | custom-call | tf_op jit(solution)/shard_map/vmap(jit(_solve_triangular))/triangular_solve | solution.py:18
  549.4 0.6 convolution_bitcast_fusion
  550.0 1.0 copy.7
  (17 shorter events, 0.5 us)
Async XLA Ops:
  7.2 27.9 %all-gather.2.cloned.1.call-start = ((), (), s32[]{:S(2)}) async-start(), calls=%async_computation.1 | async-start | bytes 2621440 | tf_op jit(solution)/shard_map/all_gather | solution.py:43
  7.9 139.9 %all-reduce.4.cloned.1.call-start = ((), (), s32[]{:S(2)}) async-start(), calls=%async_computation.2 | async-start | bytes 4194304 | tf_op jit(solution)/shard_map/psum | solution.py:44
  45.3 1.0 copy-start.2
  45.3 170.0 %all-reduce.6.cloned.1.call-start = ((), (), s32[]{:S(2)}) async-start(), calls=%async_computation.3 | async-start | bytes 4194304 | tf_op jit(solution)/shard_map/psum | solution.py:48
  164.5 286.4 %reduce-scatter.2.cloned.1.call-start = ((), (), s32[]{:S(2)}) async-start(), calls=%async_computation.4 | async-start | bytes 2621440 | tf_op jit(solution)/shard_map/reduce_scatter | solution.py:52
  225.0 47.2 %collective-permute-start = (f32[1024,512]{0,1:T(8,128)S(1)}, f32[1024,512]{0,1:T(8,128)S(1)}, u32[]{:S(2)}, u32[]{:S(2)}) collective-permute-start(f32[1024,512]{0,1:T(8,128)S(1)} %multiply_bitcast_fusion), channel_id=1, source_target_pairs={{0,4},{4,0},{8,12},{12,8},{16,20},{20,16},{24,28},{28,24},{1,5},{5... | collective-permute-start | bytes 6291464 | tf_op jit(solution)/shard_map/ppermute | solution.py:13
  272.7 138.1 %copy-start = (f32[1024,1024]{1,0:T(8,128)S(1)}, f32[1024,1024]{1,0:T(8,128)}, u32[]{:S(2)}) copy-start(f32[1024,1024]{1,0:T(8,128)} %param.2) | copy-start | bytes 12582916
  272.7 46.3 %collective-permute-start.1 = (f32[1024,512]{0,1:T(8,128)S(1)}, f32[1024,512]{0,1:T(8,128)S(1)}, u32[]{:S(2)}, u32[]{:S(2)}) collective-permute-start(f32[1024,512]{0,1:T(8,128)S(1)} %add.34), channel_id=1, source_target_pairs={{0,8},{4,12},{8,0},{12,4},{16,24},{20,28},{24,16},{28,20},{1,9},{5... | collective-permute-start | bytes 6291464 | tf_op jit(solution)/shard_map/ppermute | solution.py:13
  319.5 91.3 %collective-permute-start.2 = (f32[1024,512]{0,1:T(8,128)S(1)}, f32[1024,512]{0,1:T(8,128)S(1)}, u32[]{:S(2)}, u32[]{:S(2)}) collective-permute-start(f32[1024,512]{0,1:T(8,128)S(1)} %add.35), channel_id=1, source_target_pairs={{0,16},{4,20},{8,24},{12,28},{16,0},{20,4},{24,8},{28,12},{1,17},{... | collective-permute-start | bytes 6291464 | tf_op jit(solution)/shard_map/ppermute | solution.py:13
  419.1 31.8 %copy-start.1 = (f32[1024,512]{0,1:T(8,128)S(1)}, f32[1024,512]{0,1:T(8,128)}, u32[]{:S(2)}) copy-start(f32[1024,512]{0,1:T(8,128)} %all-reduce.6.cloned.1.call-done) | copy-start | bytes 6291460
  419.1 104.9 %all-reduce.8.cloned.1.call-start = ((), (), s32[]{:S(2)}) async-start(), calls=%async_computation.5 | async-start | bytes 131072 | tf_op jit(solution)/shard_map/psum | solution.py:56
  450.9 98.5 %copy-start.3 = (f32[1024,128]{0,1:T(8,128)S(1)}, f32[1024,128]{0,1:T(8,128)}, u32[]{:S(2)}) copy-start(f32[1024,128]{0,1:T(8,128)} %reduce-scatter.2.cloned.1.call-done) | copy-start | bytes 1572868
Sparse Core Ops, SparseCore 0:
  9.5 25.5 all-gather.1
  45.4 102.3 all-reduce.3
  164.6 50.6 all-reduce.5
  419.2 31.6 reduce-scatter.1
  454.7 69.2 all-reduce.7
